TPU v7x, 8 devices: a whole 2x2x1 slice. The times are simulated.
8 devices in a mesh: sp: 2 (over z, y), tp: 4 (over x, core).
Axes of the slice: x: 2, y: 2, z: 1, core: 2. Of those that a mesh axis runs over, the one named last changes fastest.
Arguments:
- tokens: bfloat16 [512, 5120], P('sp')
- context: bfloat16 [512, 5120], replicated
- modulation: float32 [1, 6, 5120], replicated
- w_qkv: bfloat16 [1, 5120, 3, 40, 128], P(None, None, None, 'tp')
- w_out: bfloat16 [1, 40, 128, 5120], P(None, 'tp')
- w_xq: bfloat16 [1, 5120, 40, 128], P(None, None, 'tp')
- w_xkv: bfloat16 [1, 5120, 2, 40, 128], P(None, None, None, 'tp')
- w_xout: bfloat16 [1, 40, 128, 5120], P(None, 'tp')
- w_up: bfloat16 [1, 5120, 20480], P(None, None, 'tp')
- w_down: bfloat16 [1, 20480, 5120], P(None, 'tp')
- w_final: bfloat16 [5120, 64], replicated
Outputs:
- output: float32 [512, 64], P('sp')
All inputs are finite; a program needn't handle non-finite values.
Results may differ from a plain program's by a relative error of at most 0.00672741.
Values are sent between devices in bfloat16 or wider.
A program may use at most 1 GiB of HBM per device.

v0:
```python
import math
import jax
import jax.numpy as jnp
from jax import lax
from jax.sharding import PartitionSpec as P

LN_EPS = 1e-6


def layer_norm(x_rows):
    row_mean = jnp.mean(x_rows, axis=-1, keepdims=True)
    centred = x_rows - row_mean
    row_var = jnp.mean(centred * centred, axis=-1, keepdims=True)
    return centred * lax.rsqrt(row_var + LN_EPS)


def attend(q_rows, k_rows, v_rows):
    seq_len, n_heads, head_dim = q_rows.shape
    block_len = math.gcd(seq_len, 512)
    score_scale = head_dim ** -0.5
    q_blocks = q_rows.reshape(seq_len // block_len, block_len, n_heads, head_dim)

    def per_block(q_tile):
        scores = jnp.einsum('qhd,khd->hqk', q_tile, k_rows, preferred_element_type=jnp.float32) * score_scale
        row_probs = jnp.exp(scores - jnp.max(scores, axis=-1, keepdims=True))
        row_total = jnp.sum(row_probs, axis=-1)
        mixed_out = jnp.einsum('hqk,khd->qhd', row_probs.astype(jnp.bfloat16), v_rows, preferred_element_type=jnp.float32)
        return (mixed_out / jnp.transpose(row_total)[:, :, None]).astype(jnp.bfloat16)

    return lax.map(per_block, q_blocks).reshape(seq_len, n_heads, head_dim)


def solution(mesh):
    def device_step(tokens, context, modulation, w_qkv, w_out, w_xq, w_xkv, w_xout, w_up, w_down, w_final):
        x_res = tokens.astype(jnp.float32)
        for layer_idx in range(modulation.shape[0]):
            layer_mod = modulation[layer_idx]
            h_in = (layer_norm(x_res) * (1.0 + layer_mod[1]) + layer_mod[0]).astype(jnp.bfloat16)
            qkv_local = jnp.einsum('sd,dchk->schk', h_in, w_qkv[layer_idx], preferred_element_type=jnp.float32).astype(jnp.bfloat16)
            qkv_full = lax.all_to_all(qkv_local, 'sp', 2, 0, tiled=True)
            self_full = attend(qkv_full[:, 0], qkv_full[:, 1], qkv_full[:, 2])
            self_local = lax.all_to_all(self_full, 'sp', 0, 1, tiled=True)
            self_part = jnp.einsum('shk,hkd->sd', self_local, w_out[layer_idx], preferred_element_type=jnp.float32)
            self_proj = lax.psum(self_part, 'tp').astype(jnp.bfloat16)
            x_res = x_res + layer_mod[2] * self_proj.astype(jnp.float32)
            cross_in = layer_norm(x_res).astype(jnp.bfloat16)
            cross_q = jnp.einsum('sd,dhk->shk', cross_in, w_xq[layer_idx], preferred_element_type=jnp.float32).astype(jnp.bfloat16)
            cross_kv = jnp.einsum('td,dchk->tchk', context, w_xkv[layer_idx], preferred_element_type=jnp.float32).astype(jnp.bfloat16)
            cross_out = attend(cross_q, cross_kv[:, 0], cross_kv[:, 1])
            cross_part = jnp.einsum('shk,hkd->sd', cross_out, w_xout[layer_idx], preferred_element_type=jnp.float32)
            cross_proj = lax.psum(cross_part, 'tp').astype(jnp.bfloat16)
            x_res = x_res + cross_proj.astype(jnp.float32)
            mlp_in = (layer_norm(x_res) * (1.0 + layer_mod[4]) + layer_mod[3]).astype(jnp.bfloat16)
            hidden = jax.nn.gelu(jnp.dot(mlp_in, w_up[layer_idx], preferred_element_type=jnp.float32), approximate=True).astype(jnp.bfloat16)
            mlp_part = jnp.dot(hidden, w_down[layer_idx], preferred_element_type=jnp.float32)
            mlp_out = lax.psum(mlp_part, 'tp').astype(jnp.bfloat16)
            x_res = x_res + layer_mod[5] * mlp_out.astype(jnp.float32)
        final_in = layer_norm(x_res).astype(jnp.bfloat16)
        return jnp.dot(final_in, w_final, preferred_element_type=jnp.float32)

    in_specs = (P('sp', None), P(), P(), P(None, None, None, 'tp', None), P(None, 'tp', None, None), P(None, None, 'tp', None), P(None, None, None, 'tp', None), P(None, 'tp', None, None), P(None, None, 'tp'), P(None, 'tp', None), P())
    return jax.shard_map(device_step, mesh=mesh, in_specs=in_specs, out_specs=P('sp', None), check_vma=False)
```

profile of v0, /device:TPU:0, one launch (start us, length us, event | category | flops | bytes accessed | tf_op | source)
XLA Modules:
  0.0 473.4 jit_solution(6684320114095717937)
XLA Ops:
  0.0 2.3 convert_reduce_fusion
  2.4 2.6 fusion.22
  4.9 0.6 fusion.123
  5.6 18.0 %fusion.85 = bf16[256,3,10,128]{3,0,2,1:T(8,128)(2,1)} fusion(bf16[1,5120,3,10,128]{4,1,3,2,0:T(8,128)(2,1)} %param.14, bf16[256,5120]{1,0:T(8,128)(2,1)S(1)} %copy-done.1, f32[5120]{0:T(1024)S(1)} %bitcast.133, f32[5120]{0:T(1024)S(1)} %bitcast.134, f32[256]{0:T(256)S(1)} %add_rsqrt_fusion.3, f32[256]{0:T(256)S(1)} %broadcast_multiply_fusion.3), kind=kOutput, calls=%fused_computation.79 | convolution fusion | flops 10075176960 | bytes 43952128 | tf_op jit(solution)/shard_map/sd,dchk->schk/dot_general | solution.py:39
  23.6 1.7 copy.17
  25.2 27.9 %all_to_all.36 = bf16[256,3,10,128]{3,0,1,2:T(8,128)(2,1)S(1)} all-to-all(bf16[256,3,10,128]{3,0,1,2:T(8,128)(2,1)S(1)} %copy.17), channel_id=1, replica_groups=mesh['sp'=2,'tp'=4] {'sp'}, dimensions={2} | all-to-all | bytes 3932160 | tf_op jit(solution)/shard_map/all_to_all | solution.py:40
  53.1 0.1 copy.18
  53.3 0.9 multiply_reduce_fusion.4
  54.1 0.9 fusion.39
  55.0 1.9 divide_convert_fusion.1
  56.9 2.4 copy.21
  59.3 4.6 all-to-all-start.1
  63.9 22.5 %fusion.80 = bf16[512,2,10,128]{3,0,2,1:T(8,128)(2,1)} fusion(bf16[5120,2,10,128]{3,1,2,0:T(2,128)(2,1)} %bitcast.137, bf16[512,5120]{1,0:T(8,128)(2,1)} %param.12), kind=kOutput, calls=%fused_computation.78 | convolution fusion | flops 13423083520 | bytes 34078720 | tf_op jit(solution)/shard_map/td,dchk->tchk/dot_general | solution.py:48
  86.4 0.0 all-to-all-done.1
  86.4 1.3 copy.22
  87.7 8.2 %fusion.14 = f32[256,5120]{1,0:T(8,128)} fusion(bf16[256,10,128]{2,0,1:T(8,128)(2,1)S(1)} %bitcast.125, bf16[1,10,128,5120]{3,2,1,0:T(8,128)(2,1)} %param.15), kind=kOutput, calls=%fused_computation.18 | convolution fusion | flops 3355443200 | bytes 19005440 | tf_op jit(solution)/shard_map/shk,hkd->sd/dot_general | solution.py:43
  95.9 93.7 %all-reduce.3 = bf16[256,5120]{1,0:T(8,128)(2,1)} all-reduce(f32[256,5120]{1,0:T(8,128)} %fusion.14), channel_id=1, replica_groups=mesh['sp'=2,'tp'=4] {'tp'}, use_global_device_ids=true, to_apply=%region_4.0 | all-reduce | flops 1310720 | bytes 7864320 | tf_op jit(solution)/shard_map/psum | solution.py:44
  189.6 2.8 fusion.45
  192.5 1.3 multiply_reduce_fusion.2
  193.8 12.8 %multiply_reduce_fusion.3 = (f32[10,256]{1,0:T(8,128)S(1)}, f32[10,256,512]{2,1,0:T(8,128)}) fusion(bf16[512,2,10,128]{3,0,2,1:T(8,128)(2,1)} %fusion.80, bf16[1,5120,10,128]{3,1,2,0:T(8,128)(2,1)} %param.16, bf16[256,5120]{1,0:T(8,128)(2,1)} %all-reduce.3, bf16[256,5120]{1,0:T(8,128)(2,1)S(1)} %copy-done.1, f32[256]{0:T(256)S(1)} %add_rsqrt_fusion.2, ...), kind=kOutput, calls=%fused_computation.45 | convolution fusion | flops 3703109120 | bytes 24936448 | tf_op jit(solution)/shard_map/while/body/eval_jaxpr/qhd,khd->hqk/dot_general | solution.py:24
  206.5 3.2 fusion.41
  209.8 13.8 %fusion.17 = f32[256,5120]{1,0:T(8,128)} fusion(bf16[1,10,128,5120]{3,2,1,0:T(8,128)(2,1)} %param.18, bf16[512,2,10,128]{3,0,2,1:T(8,128)(2,1)} %fusion.80, f32[10,256,512]{2,1,0:T(8,128)} %get-tuple-element.48, f32[10,256]{1,0:T(8,128)S(1)} %get-tuple-element.47, f32[256,10]{0,1:T(8,128)S(1)} %bitcast.136), kind=kOutput, calls=%fused_computation.19 | convolution fusion | flops 3695575040 | bytes 24924160 | tf_op jit(solution)/shard_map/shk,hkd->sd/dot_general | solution.py:50
  223.5 95.8 %all-reduce.4 = bf16[256,5120]{1,0:T(8,128)(2,1)} all-reduce(f32[256,5120]{1,0:T(8,128)} %fusion.17), channel_id=1, replica_groups=mesh['sp'=2,'tp'=4] {'tp'}, use_global_device_ids=true, to_apply=%region_9.10 | all-reduce | flops 1310720 | bytes 7864320 | tf_op jit(solution)/shard_map/psum | solution.py:51
  319.3 3.8 fusion.122
  323.1 2.3 copy-done.2
  325.4 0.7 multiply_reduce_fusion.1
  326.1 24.3 %fusion.35.clone.4 = bf16[256,5120]{1,0:T(8,128)(2,1)S(1)} fusion(bf16[1,5120,5120]{2,1,0:T(8,128)(2,1)} %param.19, f32[256,5120]{1,0:T(8,128)} %copy-done.2, f32[5120]{0:T(1024)S(1)} %bitcast.131, f32[5120]{0:T(1024)S(1)} %bitcast.132, f32[256]{0:T(256)S(1)} %add_rsqrt_fusion.1, f32[256]{0:T(256)S(1)} %broadcast_multiply_fusion.1), kind=kOutput, calls=%fused_computation.33.clone.clone.clone.1 | convolution fusion | flops 13440122880 | bytes 60336128 | tf_op jit(solution)/shard_map/dot_general | solution.py:54
  350.4 23.0 %fusion = f32[256,5120]{1,0:T(8,128)} fusion(bf16[1,5120,5120]{2,1,0:T(8,128)(2,1)} %param.20, bf16[256,5120]{1,0:T(8,128)(2,1)S(1)} %fusion.35.clone.4), kind=kOutput, calls=%fused_computation | convolution fusion | flops 13421772800 | bytes 60293120 | tf_op jit(solution)/shard_map/dot_general | solution.py:55
  373.4 93.8 %all-reduce.5 = bf16[256,5120]{1,0:T(8,128)(2,1)S(1)} all-reduce(f32[256,5120]{1,0:T(8,128)} %fusion), channel_id=1, replica_groups=mesh['sp'=2,'tp'=4] {'tp'}, use_global_device_ids=true, to_apply=%region_12.13 | all-reduce | flops 1310720 | bytes 7864320 | tf_op jit(solution)/shard_map/psum | solution.py:56
  467.3 3.3 fusion.121
  470.6 0.7 multiply_reduce_fusion
  471.2 1.7 fusion.52
  (19 shorter events, 0.1 us)
Async XLA Ops:
  0.0 471.2 %copy-start = (bf16[5120,64]{0,1:T(8,128)(2,1)S(1)}, bf16[5120,64]{0,1:T(8,128)(2,1)}, u32[]{:S(2)}) copy-start(bf16[5120,64]{0,1:T(8,128)(2,1)} %param.21) | copy-start | bytes 1966084
  0.0 5.6 %copy-start.1 = (bf16[256,5120]{1,0:T(8,128)(2,1)S(1)}, bf16[256,5120]{1,0:T(8,128)(2,1)}, u32[]{:S(2)}) copy-start(bf16[256,5120]{1,0:T(8,128)(2,1)} %param.11) | copy-start | bytes 7864324
  0.0 4.9 %copy-start.4 = (f32[1,6,5120]{2,0,1:T(1,128)S(1)}, f32[1,6,5120]{2,0,1:T(1,128)}, u32[]{:S(2)}) copy-start(f32[1,6,5120]{2,0,1:T(1,128)} %param.13) | copy-start | bytes 368644
  59.3 27.1 %all-to-all-start.1 = ((bf16[512,5,128]{2,1,0:T(8,128)(2,1)}), bf16[512,5,128]{2,1,0:T(8,128)(2,1)}, u32[]{:S(2)}, u32[]{:S(2)}) async-start(bf16[512,5,128]{2,1,0:T(8,128)(2,1)} %copy.21), calls=%async_computation.1 | async-start | bytes 2097152 | tf_op jit(solution)/shard_map/all_to_all | solution.py:42
  189.6 2.8 copy-start.3
  323.1 2.3 copy-start.2
  373.4 93.9 %copy-start.5 = (f32[1,1,5120]{2,0,1:T(1,128)S(1)}, f32[1,1,5120]{2,0,1:T(1,128)}, u32[]{:S(2)}) copy-start(f32[1,1,5120]{2,0,1:T(1,128)} %get-tuple-element.32) | copy-start | bytes 61444
where the time goes:
time: 480 us; the launch traced here: 473 us
  blocking collectives  311 us (65%)
  matrix products  127 us (26%)
  other arithmetic  22.2 us (5%)
  local copies, waits for them, and re-layouts  7.81 us (2%)
    psum x1, blocking collectives, device_step(): cross_proj = lax.psum(cross_part, 'tp').astype(jnp.bfloat16)  95.8 us
    psum x1, blocking collectives, device_step(): mlp_out = lax.psum(mlp_part, 'tp').astype(jnp.bfloat16)  93.8 us
    psum x1, blocking collectives, device_step(): self_proj = lax.psum(self_part, 'tp').astype(jnp.bfloat16)  93.7 us
    all_to_all x1, blocking collectives, device_step(): qkv_full = lax.all_to_all(qkv_local, 'sp', 2, 0, tiled=True)  27.9 us
    dot_general x1, matrix products, device_step(): jnp.dot(mlp_in, w_up[layer_idx], preferred_element_type=jnp.float32)  24.3 us
    dot_general x1, matrix products, device_step(): jnp.dot(hidden, w_down[layer_idx], preferred_element_type=jnp.float32)  23 us
    dot_general x1, matrix products, device_step(): jnp.einsum('td,dchk->tchk', context, w_xkv[layer_idx], preferred_element_...  22.5 us
    dot_general x1, matrix products, device_step(): jnp.einsum('sd,dchk->schk', h_in, w_qkv[layer_idx], preferred_element_typ...  18 us
  transfers between devices with their start and end apart: 1, of which 0 were waited for; matrix products, arithmetic and copies ran while one was open for 5% of the time, Pallas kernels for 0%

commit v1 on v0

v1 whole, which is shorter than its diff:
```python
import functools
import jax
import jax.numpy as jnp
from jax import lax
from jax.experimental import pallas as pl
from jax.experimental.pallas import tpu as pltpu
from jax.sharding import PartitionSpec as P

F32 = jnp.float32
BF16 = jnp.bfloat16
LN_EPS = 1e-6
MESH = pl.DeviceIdType.MESH

D = 5120
ROWS = 256
NT = 20
KC = 4
HL = 10
NH = 2
RH = ROWS // NH
CB = RH // 2
OB = RH // 4
NSLOT = 40
HALVES = tuple(range(NH))


def dot(a, b):
    return jnp.dot(a, b, preferred_element_type=F32)


def dot_nt(a, b):
    return lax.dot_general(a, b, (((1,), (1,)), ((), ())), preferred_element_type=F32)


def block_kernel(q_hbm, kv_hbm, kvo_hbm, xkv_hbm, tok_hbm, mod_ref, w_out, w_xq, w_xout, w_up, w_down, wf_hbm,
                 out_ref,
                 ring, part, dsum, xin, xres, hbuf, ubuf, qacc, obuf, qbuf, kvs, kvx, tok, wf, obout,
                 rsem, lsem, ds_s, ds_r, xs_s, xs_r, ax_s, ax_r, ad_s, ad_r, af_s, af_r, os_s, os_r):
    sp = lax.axis_index('sp')
    tp = lax.axis_index('tp')
    x = tp // 2
    c = tp % 2
    partner = (sp, 2 * x + (1 - c))
    across = (sp, 2 * (1 - x) + c)
    diagonal = (sp, 2 * (1 - x) + (1 - c))

    def kslice(kc):
        return pl.ds(kc * 1280, 1280)

    def nslice(nb):
        return pl.ds(nb * 256, 256)

    def start_cols(w, kc, nb, slot):
        pltpu.make_async_copy(w.at[kslice(kc), nslice(nb)], ring.at[slot], rsem.at[slot]).start()

    def start_xq(kc, b, slot):
        for hh in range(2):
            pltpu.make_async_copy(w_xq.at[2 * b + hh, kslice(kc), :], ring.at[slot, :, pl.ds(128 * hh, 128)],
                                  rsem.at[slot]).start()

    def wait_block(slot):
        pltpu.make_async_copy(w_out.at[pl.ds(0, 1280), pl.ds(0, 256)], ring.at[slot], rsem.at[slot]).wait()

    def start_down(g, i, slot):
        start_cols(w_down, i % 4, 5 * g + i // 4, slot)

    own_rows = [a * RH + c * CB + x * OB for a in HALVES]
    loads = [
        (q_hbm, qbuf, 0),
        (kv_hbm, kvs.at[:, :, pl.ds(0, 256), :], 1),
        (kvo_hbm, kvs.at[:, :, pl.ds(256, 256), :], 2),
        (xkv_hbm, kvx, 3),
        (wf_hbm, wf, 4),
    ] + [(tok_hbm.at[pl.ds(pl.multiple_of(own_rows[a], OB), OB), :], tok.at[a], 5 + a) for a in HALVES]

    def load(i):
        s, d, k = loads[i]
        return pltpu.make_async_copy(s, d, lsem.at[k])

    for i in range(3):
        load(i).start()

    @pl.loop(0, NT)
    def _(t):
        start_cols(w_out, 0, t, t)

    for i in range(3, len(loads)):
        load(i).start()

    @pl.loop(0, NT)
    def _(i):
        start_xq(i // 5, i % 5, 20 + i)

    barrier = pltpu.get_barrier_semaphore()
    for peer in (partner, across, diagonal):
        pl.semaphore_signal(barrier, inc=1, device_id=peer, device_id_type=MESH)

    scale = 128 ** -0.5

    def attend(qh, kv, h):
        s1 = dot_nt(qh, kv[0, h, 0:256, :]) * scale
        s2 = dot_nt(qh, kv[0, h, 256:512, :]) * scale
        m = jnp.maximum(jnp.max(s1, axis=-1, keepdims=True), jnp.max(s2, axis=-1, keepdims=True))
        p1 = jnp.exp(s1 - m)
        p2 = jnp.exp(s2 - m)
        total = jnp.sum(p1, axis=-1, keepdims=True) + jnp.sum(p2, axis=-1, keepdims=True)
        o = dot(p1.astype(BF16), kv[1, h, 0:256, :]) + dot(p2.astype(BF16), kv[1, h, 256:512, :])
        return (o / total).astype(BF16)

    def d2d(a, t):
        src = part.at[t, pl.ds(pl.multiple_of(a * RH + (1 - c) * CB, OB), CB), :]
        return pltpu.make_async_remote_copy(src_ref=src, dst_ref=dsum.at[a, t], send_sem=ds_s.at[a, t],
                                            recv_sem=ds_r.at[a, t], device_id=partner, device_id_type=MESH)

    def xsend(a, t):
        src = dsum.at[a, t, pl.ds(pl.multiple_of((1 - x) * OB, OB), OB), :]
        return pltpu.make_async_remote_copy(src_ref=src, dst_ref=xin.at[a, t], send_sem=xs_s.at[a, t],
                                            recv_sem=xs_r.at[a, t], device_id=across, device_id_type=MESH)

    def core_sum(a, t):
        d2d(a, t).wait_recv()
        dsum[a, t] = dsum[a, t] + part[t, pl.ds(pl.multiple_of(a * RH + c * CB, OB), CB), :]

    def rs_loop(compute, compute_halves, send_halves, per_iter, lag):
        iters = NT // per_iter

        @pl.loop(0, iters + lag)
        def _(i):
            @pl.when(i < iters)
            def _():
                for u in range(per_iter):
                    compute(i * per_iter + u)

            @pl.when(i >= lag)
            def _():
                for u in range(per_iter):
                    for a in send_halves:
                        core_sum(a, (i - lag) * per_iter + u)

            @pl.when(i < iters)
            def _():
                for u in range(per_iter):
                    for a in compute_halves:
                        d2d(a, i * per_iter + u).start()

            @pl.when(i >= lag)
            def _():
                for u in range(per_iter):
                    for a in send_halves:
                        xsend(a, (i - lag) * per_iter + u).start()

    def hrows(core, chip, a):
        return pl.ds(pl.multiple_of(a * RH + core * CB + chip * OB, OB), OB)

    def gather_copy(kc, rows, ssem, rsem_, peer):
        ref = hbuf.at[pl.ds(kc * 5, 5), rows, :]
        return pltpu.make_async_remote_copy(src_ref=ref, dst_ref=ref, send_sem=ssem, recv_sem=rsem_,
                                            device_id=peer, device_id_type=MESH)

    def g_across(a, kc, chip):
        return gather_copy(kc, hrows(c, chip, a), ax_s.at[a, kc], ax_r.at[a, kc], across)

    def g_partner(a, kc, core):
        return gather_copy(kc, hrows(core, x, a), ad_s.at[a, kc], ad_r.at[a, kc], partner)

    def g_forward(a, kc, core):
        return gather_copy(kc, hrows(core, 1 - x, a), af_s.at[a, kc], af_r.at[a, kc], partner)

    def modrow(r, t):
        return mod_ref[r, 0:1, pl.ds(pl.multiple_of(t * 256, 256), 256)]

    def residual(a, gate, first):
        def body(i, acc):
            for u in range(4):
                t = i * 4 + u
                xsend(a, t).wait()
                d2d(a, t).wait_send()
                proj = (dsum[a, t, pl.ds(pl.multiple_of(x * OB, OB), OB), :] + xin[a, t]).astype(BF16).astype(F32)
                if gate is not None:
                    proj = modrow(gate, t) * proj
                if first:
                    prev = tok[a, :, pl.ds(pl.multiple_of(t * 256, 256), 256)].astype(F32)
                else:
                    prev = xres[a, t]
                new = prev + proj
                xres[a, t] = new
                acc = acc + new
            return acc
        acc = lax.fori_loop(0, NT // 4, body, jnp.zeros((OB, 256), F32))
        return jnp.sum(acc, axis=-1, keepdims=True)

    def stats(a, row_sum):
        mean = row_sum / D

        def body(i, acc):
            for u in range(4):
                d_ = xres[a, i * 4 + u] - mean
                acc = acc + d_ * d_
            return acc
        acc = lax.fori_loop(0, NT // 4, body, jnp.zeros((OB, 256), F32))
        var = jnp.sum(acc, axis=-1, keepdims=True) / D
        return mean, lax.rsqrt(var + LN_EPS)

    def norm_and_send(a, gate, first, shift, gain):
        mean, inv = stats(a, residual(a, gate, first))

        @pl.loop(0, KC)
        def _(kc):
            for u in range(5):
                t = kc * 5 + u
                h = (xres[a, t] - mean) * inv
                if gain is not None:
                    h = h * (1.0 + modrow(gain, t)) + modrow(shift, t)
                hbuf[t, hrows(c, x, a), :] = h.astype(BF16)
            g_across(a, kc, x).start()
            g_partner(a, kc, c).start()

    def gather_forward(a, kc):
        g_across(a, kc, 1 - x).wait_recv()
        g_forward(a, kc, c).start()

    def gather_wait(a, kc):
        g_partner(a, kc, 1 - c).wait_recv()
        g_forward(a, kc, 1 - c).wait_recv()
        g_across(a, kc, x).wait_send()
        g_partner(a, kc, c).wait_send()
        g_forward(a, kc, c).wait_send()

    def mm(lhs, slot):
        acc = dot(lhs(0), ring[slot, 0:256, :])
        for j in range(1, 5):
            acc = acc + dot(lhs(j), ring[slot, 256 * j:256 * (j + 1), :])
        return acc

    for i in range(3):
        load(i).wait()

    @pl.loop(0, HL // 2)
    def _(b):
        for hh in range(2):
            for a in HALVES:
                rows = pl.ds(a * RH, RH)
                obuf[b, rows, 128 * hh:128 * (hh + 1)] = attend(qbuf[2 * b + hh, rows, :], kvs, 2 * b + hh)

    pl.semaphore_wait(barrier, 3)

    def out_tile(t):
        wait_block(t)
        part[t] = mm(lambda j: obuf[j], t)
        start_cols(w_xout, 0, t, t)

    rs_loop(out_tile, HALVES, HALVES[:1], 4, 2)
    for a in HALVES[1:]:
        @pl.loop(0, NT)
        def _(t):
            core_sum(a, t)
            xsend(a, t).start()

    for i in range(3, len(loads)):
        load(i).wait()
    for a in HALVES:
        norm_and_send(a, 2, True, None, None)

    for a in HALVES:
        rows = pl.ds(a * RH, RH)
        last = a == HALVES[-1]
        for b in range(5):
            qacc[b, rows, :] = jnp.zeros((RH, 256), F32)

        gather_forward(a, 0)

        @pl.loop(0, KC)
        def _(kc):
            @pl.when(kc < KC - 1)
            def _():
                gather_forward(a, kc + 1)
            gather_wait(a, kc)
            for b in range(5):
                slot = 20 + kc * 5 + b
                if a == 0:
                    wait_block(slot)
                qacc[b, rows, :] += mm(lambda j: hbuf[kc * 5 + j, rows, :], slot)
                if last:
                    start_cols(w_up, 0, kc * 5 + b, slot)

        @pl.loop(0, HL // 2)
        def _(b):
            for hh in range(2):
                qh = qacc[b, rows, 128 * hh:128 * (hh + 1)].astype(BF16)
                obuf[b, rows, 128 * hh:128 * (hh + 1)] = attend(qh, kvx, 2 * b + hh)

        def xout_tile(t):
            if a == 0:
                wait_block(t)
            part[t, rows, :] = mm(lambda j: obuf[j, rows, :], t)
            if last:
                start_cols(w_up, 1, t, t)

        rs_loop(xout_tile, (a,), (a,), 4, 2)

    for a in HALVES:
        norm_and_send(a, None, False, 3, 4)

    for a in HALVES[:-1]:
        @pl.loop(0, KC)
        def _(kc):
            gather_forward(a, kc)
    gather_forward(HALVES[-1], 0)
    for kc in range(KC):
        if kc < KC - 1:
            gather_forward(HALVES[-1], kc + 1)
        for a in HALVES:
            gather_wait(a, kc)
        base = 20 if kc % 2 == 0 else 0

        @pl.loop(0, NT // 4)
        def _(i):
            for u in range(4):
                nb = i * 4 + u
                wait_block(base + nb)
                acc = mm(lambda j: hbuf[kc * 5 + j], base + nb)
                if kc > 0:
                    acc = part[nb] + acc
                if kc < KC - 1:
                    part[nb] = acc
                else:
                    ubuf[nb] = jax.nn.gelu(acc, approximate=True).astype(BF16)
                if kc < 2:
                    start_cols(w_up, kc + 2, nb, base + nb)
                else:
                    start_down(kc - 2, nb, base + nb)

    def down_tile(t):
        g = t // 5
        base = 20 * ((g + 1) % 2) + 4 * (t % 5)
        acc = None
        for kc in range(KC):
            wait_block(base + kc)
            new = mm(lambda j: ubuf[5 * kc + j], base + kc)
            acc = new if acc is None else acc + new
        part[t] = acc

        @pl.when(g < 2)
        def _():
            for kc in range(KC):
                start_cols(w_down, kc, t + 10, base + kc)

    rs_loop(down_tile, HALVES, HALVES, 1, 2)

    def out_copy(a, peer, k, core, chip):
        ref = obout.at[hrows(core, chip, a), :]
        return pltpu.make_async_remote_copy(src_ref=ref, dst_ref=ref, send_sem=os_s.at[a, k], recv_sem=os_r.at[a, k],
                                            device_id=peer, device_id_type=MESH)

    for a in HALVES:
        mean, inv = stats(a, residual(a, 5, False))

        def body(i, acc):
            for u in range(4):
                t = i * 4 + u
                fin = ((xres[a, t] - mean) * inv).astype(BF16)
                acc = acc + dot_nt(fin, wf[:, pl.ds(pl.multiple_of(t * 256, 256), 256)])
            return acc
        acc = lax.fori_loop(0, NT // 4, body, jnp.zeros((OB, 64), F32))
        obout[hrows(c, x, a), :] = jnp.concatenate([acc, jnp.zeros((OB, 64), F32)], axis=1)
        out_copy(a, across, 0, c, x).start()
        out_copy(a, partner, 1, c, x).start()
        out_copy(a, diagonal, 2, c, x).start()
    for a in HALVES:
        out_copy(a, across, 0, c, 1 - x).wait()
        out_copy(a, partner, 1, 1 - c, x).wait()
        out_copy(a, diagonal, 2, 1 - c, 1 - x).wait()
    out_ref[...] = obout[:, 0:64]


def block_call(args):
    any_spec = pl.BlockSpec(memory_space=pl.ANY)
    vmem_spec = pl.BlockSpec(memory_space=pltpu.VMEM)
    sem = pltpu.SemaphoreType.DMA
    return pl.pallas_call(
        block_kernel,
        out_shape=jax.ShapeDtypeStruct((ROWS, 64), F32),
        in_specs=[any_spec] * 5 + [vmem_spec] + [any_spec] * 6,
        out_specs=vmem_spec,
        scratch_shapes=[
            pltpu.VMEM((NSLOT, 1280, 256), BF16),
            pltpu.VMEM((NT, ROWS, 256), F32),
            pltpu.VMEM((NH, NT, CB, 256), F32),
            pltpu.VMEM((NH, NT, OB, 256), F32),
            pltpu.VMEM((NH, NT, OB, 256), F32),
            pltpu.VMEM((NT, ROWS, 256), BF16),
            pltpu.VMEM((NT, ROWS, 256), BF16),
            pltpu.VMEM((5, ROWS, 256), F32),
            pltpu.VMEM((5, ROWS, 256), BF16),
            pltpu.VMEM((HL, ROWS, 128), BF16),
            pltpu.VMEM((2, HL, 512, 128), BF16),
            pltpu.VMEM((2, HL, 512, 128), BF16),
            pltpu.VMEM((NH, OB, D), BF16),
            pltpu.VMEM((64, D), BF16),
            pltpu.VMEM((ROWS, 128), F32),
            sem((NSLOT,)), sem((8,)),
            sem((NH, NT)), sem((NH, NT)), sem((NH, NT)), sem((NH, NT)),
            sem((NH, KC)), sem((NH, KC)), sem((NH, KC)), sem((NH, KC)), sem((NH, KC)), sem((NH, KC)),
            sem((NH, 3)), sem((NH, 3)),
        ],
        compiler_params=pltpu.CompilerParams(collective_id=0, has_side_effects=True, vmem_limit_bytes=63 * 2**20),
        cost_estimate=pl.CostEstimate(flops=2 * 256 * 72 * 10**6, bytes_accessed=150 * 10**6, transcendentals=4 * 10**6),
        name='dit_block',
    )(*args)


def layer_norm(x_rows):
    row_mean = jnp.mean(x_rows, axis=-1, keepdims=True)
    centred = x_rows - row_mean
    row_var = jnp.mean(centred * centred, axis=-1, keepdims=True)
    return centred * lax.rsqrt(row_var + LN_EPS)


def solution(mesh):
    def device_step(tokens, context, modulation, w_qkv, w_out, w_xq, w_xkv, w_xout, w_up, w_down, w_final):
        mod = modulation[0]
        h_in = (layer_norm(tokens.astype(F32)) * (1.0 + mod[1]) + mod[0]).astype(BF16)
        kv = jnp.einsum('sd,dchk->schk', h_in, w_qkv[0][:, 1:3], preferred_element_type=F32).astype(BF16)
        kv = jnp.transpose(kv, (1, 2, 0, 3))
        kv_other = lax.ppermute(kv, 'sp', [(0, 1), (1, 0)])
        q = jnp.einsum('sd,dhk->shk', h_in, w_qkv[0][:, 0], preferred_element_type=F32).astype(BF16)
        q = jnp.transpose(q, (1, 0, 2))
        xkv = jnp.einsum('td,dchk->tchk', context, w_xkv[0], preferred_element_type=F32).astype(BF16)
        xkv = jnp.transpose(xkv, (1, 2, 0, 3))
        return block_call((
            q, kv, kv_other, xkv, tokens, jnp.transpose(modulation, (1, 0, 2)),
            w_out[0].reshape(1280, D), jnp.transpose(w_xq[0], (1, 0, 2)), w_xout[0].reshape(1280, D),
            w_up[0], w_down[0], jnp.transpose(w_final)))

    in_specs = (P('sp', None), P(), P(), P(None, None, None, 'tp', None), P(None, 'tp', None, None),
                P(None, None, 'tp', None), P(None, None, None, 'tp', None), P(None, 'tp', None, None),
                P(None, None, 'tp'), P(None, 'tp', None), P())
    return jax.shard_map(device_step, mesh=mesh, in_specs=in_specs, out_specs=P('sp', None), check_vma=False)
```

time: 480 us -> 248 us (0.52); the launches traced: 473 us -> 247 us
  blocking collectives: 311 us -> 0 us
  Pallas kernels: 0 us -> 192 us
  matrix products: 127 us -> 44.5 us
  other arithmetic: 22.2 us -> 5.68 us
  local copies, waits for them, and re-layouts: 7.81 us -> 1.63 us
    psum x3 -> x0, blocking collectives: 283 us -> none  [the longest x1 95.8 us: device_step(): cross_proj = lax.psum(cross_part, 'tp').astype(jnp.bfloat16)]
    pallas_call x0 -> x1, Pallas kernels: none -> 192 us  [block_call(): pl.pallas_call(block_kernel, out_shape=jax.ShapeDtypeStruct((ROWS, 64), F...]
    dot_general x10 -> x3, matrix products: 127 us -> 44.5 us  [the longest x1 22.4 us: device_step(): jnp.einsum('td,dchk->tchk', context, w_xkv[0], preferred_element_type=F32)]
    all_to_all x1 -> x0, blocking collectives: 27.9 us -> none  [device_step(): qkv_full = lax.all_to_all(qkv_local, 'sp', 2, 0, tiled=True)]
    reduce_sum x4 -> x1, other arithmetic: 12.2 us -> 2.32 us  [layer_norm(): row_mean = jnp.mean(x_rows, axis=-1, keepdims=True)]
  transfers between devices with their start and end apart: 1 -> 1, of which waited for: 0 -> 0; matrix products, arithmetic and copies ran while one was open for 5% -> 13% of each run, Pallas kernels for 0% -> 0%
where the time goes in v1:
time: 248 us; the launch traced here: 247 us
  Pallas kernels  192 us (77%)
  matrix products  44.5 us (18%)
  other arithmetic  5.68 us (2%)
  starting transfers between devices  3.39 us (1%)
    pallas_call x1, Pallas kernels, block_call(): pl.pallas_call(block_kernel, out_shape=jax.ShapeDtypeStruct((ROWS, 64), F...  192 us
    dot_general x1, matrix products, device_step(): jnp.einsum('td,dchk->tchk', context, w_xkv[0], preferred_element_type=F32)  22.4 us
    dot_general x1, matrix products, device_step(): jnp.einsum('sd,dchk->schk', h_in, w_qkv[0][:, 1:3], preferred_element_typ...  12.6 us
    dot_general x1, matrix products, device_step(): jnp.einsum('sd,dhk->shk', h_in, w_qkv[0][:, 0], preferred_element_type=F32)  9.48 us
  transfers between devices with their start and end apart: 1, of which 0 were waited for; matrix products, arithmetic and copies ran while one was open for 13% of the time, Pallas kernels for 0%

profile of v1, /device:TPU:0, one launch (start us, length us, event | category | flops | bytes accessed | tf_op | source)
XLA Modules:
  0.0 247.4 jit_solution(4161399734034845835)
XLA Ops:
  0.0 0.0 copy-start
  0.0 2.3 convert_reduce_fusion
  2.3 2.6 %fusion.7 = f32[256]{0:T(256)S(1)} fusion(bf16[256,5120]{1,0:T(8,128)(2,1)} %tok_hbm.1, f32[256]{0:T(256)S(1)} %broadcast_multiply_fusion), kind=kLoop, calls=%fused_computation.10 | loop fusion | flops 5242624 | bytes 2623488 | tf_op jit(solution)/shard_map/reduce_sum | solution.py:415
  4.9 0.8 slice_add_fusion
  5.7 0.0 copy-done
  5.7 12.6 %fusion.23.kv_hbm = bf16[2,10,256,128]{3,2,1,0:T(8,128)(2,1)S(1)} fusion(bf16[5120,3,10,128]{3,0,2,1:T(8,128)(2,1)} %bitcast.60, bf16[256,5120]{1,0:T(8,128)(2,1)S(1)} %copy-done, f32[5120]{0:T(1024)S(1)} %bitcast.58, f32[5120]{0:T(1024)S(1)} %bitcast.56, f32[256]{0:T(256)S(1)} %add_rsqrt_fusion, f32[256]{0:T(256)S(1)} %broadcast_multiply_fusion), kind=kOutput, calls=%fused_computation.19 | convolution fusion | flops 6719406080 | bytes 30189568 | tf_op jit(solution)/shard_map/sd,dchk->schk/dot_general | solution.py:423
  18.3 0.0 copy-start.1
  18.3 3.4 %collective-permute-start = (bf16[2,10,256,128]{3,2,1,0:T(8,128)(2,1)S(1)}, bf16[2,10,256,128]{3,2,1,0:T(8,128)(2,1)}, u32[]{:S(2)}, u32[]{:S(2)}) collective-permute-start(bf16[2,10,256,128]{3,2,1,0:T(8,128)(2,1)S(1)} %fusion.23.kv_hbm), channel_id=1, source_target_pairs={{0,4},{4,0},{1,5},{5,1},{2,6},{6,2},{3,7},{7,3}} | collective-permute-start | bytes 3932168 | tf_op jit(solution)/shard_map/ppermute | solution.py:425
  21.7 22.4 %convert_bitcast_fusion.xkv_hbm = bf16[2,10,512,128]{3,2,1,0:T(8,128)(2,1)} fusion(bf16[5120,2,10,128]{3,1,2,0:T(2,128)(2,1)} %bitcast.62, bf16[512,5120]{1,0:T(8,128)(2,1)} %param.12), kind=kOutput, calls=%fused_computation.17 | convolution fusion | flops 13423083520 | bytes 34078720 | tf_op jit(solution)/shard_map/td,dchk->tchk/dot_general | solution.py:428
  44.1 0.0 copy-done.1
  44.1 9.5 %fusion.31.q_hbm = bf16[10,256,128]{2,1,0:T(8,128)(2,1)} fusion(bf16[5120,3,10,128]{3,0,2,1:T(8,128)(2,1)} %bitcast.61, bf16[256,5120]{1,0:T(8,128)(2,1)S(1)} %copy-done, f32[5120]{0:T(1024)S(1)} %bitcast.59, f32[5120]{0:T(1024)S(1)} %bitcast.57, f32[256]{0:T(256)S(1)} %add_rsqrt_fusion, f32[256]{0:T(256)S(1)} %broadcast_multiply_fusion), kind=kOutput, calls=%fused_computation.21 | convolution fusion | flops 3363635200 | bytes 16427008 | tf_op jit(solution)/shard_map/sd,dhk->shk/dot_general | solution.py:426
  53.6 0.0 collective-permute-done.kvo_hbm
  53.6 192.2 %dit_block.1 = f32[256,64]{1,0:T(8,128)} custom-call(bf16[10,256,128]{2,1,0:T(8,128)(2,1)} %fusion.31.q_hbm, bf16[2,10,256,128]{3,2,1,0:T(8,128)(2,1)} %copy-done.1, bf16[2,10,256,128]{3,2,1,0:T(8,128)(2,1)} %collective-permute-done.kvo_hbm, bf16[2,10,512,128]{3,2,1,0:T(8,128)(2,1)} %convert_bitcast_fusion.xkv_hbm, bf16[256,5120]{1,0:T(8,128)(2,1)} %tok_hbm.1, ...), custom_call_target="tpu_custom_call" | custom-call | flops 36864000000 | bytes 150000000 | tf_op jit(solution)/shard_map/dit_block/pallas_call | solution.py:380
  245.8 1.6 copy.13
  (2 shorter events, 0.0 us)
Async XLA Ops:
  0.0 5.7 %copy-start = (bf16[256,5120]{1,0:T(8,128)(2,1)S(1)}, bf16[256,5120]{1,0:T(8,128)(2,1)}, u32[]{:S(2)}) copy-start(bf16[256,5120]{1,0:T(8,128)(2,1)} %tok_hbm.1) | copy-start | bytes 7864324
  18.3 25.9 %copy-start.1 = (bf16[2,10,256,128]{3,2,1,0:T(8,128)(2,1)}, bf16[2,10,256,128]{3,2,1,0:T(8,128)(2,1)S(1)}, u32[]{:S(2)}) copy-start(bf16[2,10,256,128]{3,2,1,0:T(8,128)(2,1)S(1)} %fusion.23.kv_hbm) | copy-start | bytes 3932164
  18.3 35.3 %collective-permute-start = (bf16[2,10,256,128]{3,2,1,0:T(8,128)(2,1)S(1)}, bf16[2,10,256,128]{3,2,1,0:T(8,128)(2,1)}, u32[]{:S(2)}, u32[]{:S(2)}) collective-permute-start(bf16[2,10,256,128]{3,2,1,0:T(8,128)(2,1)S(1)} %fusion.23.kv_hbm), channel_id=1, source_target_pairs={{0,4},{4,0},{1,5},{5,1},{2,6},{6,2},{3,7},{7,3}} | collective-permute-start | bytes 3932168 | tf_op jit(solution)/shard_map/ppermute | solution.py:425

commit v2 on v1

--- a/solution.py
+++ b/solution.py
@@ -22,6 +22,8 @@
 OB = RH // 4
 NSLOT = 40
 HALVES = tuple(range(NH))
+GA = 4
+GD = 2
 
 
 def dot(a, b):
@@ -107,47 +109,45 @@
         o = dot(p1.astype(BF16), kv[1, h, 0:256, :]) + dot(p2.astype(BF16), kv[1, h, 256:512, :])
         return (o / total).astype(BF16)
 
-    def d2d(a, t):
-        src = part.at[t, pl.ds(pl.multiple_of(a * RH + (1 - c) * CB, OB), CB), :]
-        return pltpu.make_async_remote_copy(src_ref=src, dst_ref=dsum.at[a, t], send_sem=ds_s.at[a, t],
-                                            recv_sem=ds_r.at[a, t], device_id=partner, device_id_type=MESH)
-
-    def xsend(a, t):
-        src = dsum.at[a, t, pl.ds(pl.multiple_of((1 - x) * OB, OB), OB), :]
-        return pltpu.make_async_remote_copy(src_ref=src, dst_ref=xin.at[a, t], send_sem=xs_s.at[a, t],
-                                            recv_sem=xs_r.at[a, t], device_id=across, device_id_type=MESH)
-
-    def core_sum(a, t):
-        d2d(a, t).wait_recv()
-        dsum[a, t] = dsum[a, t] + part[t, pl.ds(pl.multiple_of(a * RH + c * CB, OB), CB), :]
-
-    def rs_loop(compute, compute_halves, send_halves, per_iter, lag):
-        iters = NT // per_iter
+    def d2d(a, i, g):
+        src = part.at[pl.ds(i * g, g), pl.ds(pl.multiple_of(a * RH + (1 - c) * CB, OB), CB), :]
+        return pltpu.make_async_remote_copy(src_ref=src, dst_ref=dsum.at[a, pl.ds(i * g, g)], send_sem=ds_s.at[a, i],
+                                            recv_sem=ds_r.at[a, i], device_id=partner, device_id_type=MESH)
+
+    def xsend(a, i, g):
+        src = dsum.at[a, pl.ds(i * g, g), pl.ds(pl.multiple_of((1 - x) * OB, OB), OB), :]
+        return pltpu.make_async_remote_copy(src_ref=src, dst_ref=xin.at[a, pl.ds(i * g, g)], send_sem=xs_s.at[a, i],
+                                            recv_sem=xs_r.at[a, i], device_id=across, device_id_type=MESH)
+
+    def core_sum(a, i, g):
+        d2d(a, i, g).wait_recv()
+        for u in range(g):
+            t = i * g + u
+            dsum[a, t] = dsum[a, t] + part[t, pl.ds(pl.multiple_of(a * RH + c * CB, OB), CB), :]
+
+    def rs_loop(compute, compute_halves, send_halves, g, lag):
+        iters = NT // g
 
         @pl.loop(0, iters + lag)
         def _(i):
             @pl.when(i < iters)
             def _():
-                for u in range(per_iter):
-                    compute(i * per_iter + u)
+                compute(i)
 
             @pl.when(i >= lag)
             def _():
-                for u in range(per_iter):
-                    for a in send_halves:
-                        core_sum(a, (i - lag) * per_iter + u)
+                for a in send_halves:
+                    core_sum(a, i - lag, g)
 
             @pl.when(i < iters)
             def _():
-                for u in range(per_iter):
-                    for a in compute_halves:
-                        d2d(a, i * per_iter + u).start()
+                for a in compute_halves:
+                    d2d(a, i, g).start()
 
             @pl.when(i >= lag)
             def _():
-                for u in range(per_iter):
-                    for a in send_halves:
-                        xsend(a, (i - lag) * per_iter + u).start()
+                for a in send_halves:
+                    xsend(a, i - lag, g).start()
 
     def hrows(core, chip, a):
         return pl.ds(pl.multiple_of(a * RH + core * CB + chip * OB, OB), OB)
@@ -169,12 +169,12 @@
     def modrow(r, t):
         return mod_ref[r, 0:1, pl.ds(pl.multiple_of(t * 256, 256), 256)]
 
-    def residual(a, gate, first):
+    def residual(a, gate, first, g):
         def body(i, acc):
-            for u in range(4):
-                t = i * 4 + u
-                xsend(a, t).wait()
-                d2d(a, t).wait_send()
+            xsend(a, i, g).wait()
+            d2d(a, i, g).wait_send()
+            for u in range(g):
+                t = i * g + u
                 proj = (dsum[a, t, pl.ds(pl.multiple_of(x * OB, OB), OB), :] + xin[a, t]).astype(BF16).astype(F32)
                 if gate is not None:
                     proj = modrow(gate, t) * proj
@@ -186,7 +186,7 @@
                 xres[a, t] = new
                 acc = acc + new
             return acc
-        acc = lax.fori_loop(0, NT // 4, body, jnp.zeros((OB, 256), F32))
+        acc = lax.fori_loop(0, NT // g, body, jnp.zeros((OB, 256), F32))
         return jnp.sum(acc, axis=-1, keepdims=True)
 
     def stats(a, row_sum):
@@ -202,7 +202,7 @@
         return mean, lax.rsqrt(var + LN_EPS)
 
     def norm_and_send(a, gate, first, shift, gain):
-        mean, inv = stats(a, residual(a, gate, first))
+        mean, inv = stats(a, residual(a, gate, first, GA))
 
         @pl.loop(0, KC)
         def _(kc):
@@ -244,17 +244,20 @@
 
     pl.semaphore_wait(barrier, 3)
 
-    def out_tile(t):
-        wait_block(t)
-        part[t] = mm(lambda j: obuf[j], t)
-        start_cols(w_xout, 0, t, t)
-
-    rs_loop(out_tile, HALVES, HALVES[:1], 4, 2)
+    def out_tiles(i):
+        for u in range(GA):
+            wait_block(i * GA + u)
+        for u in range(GA):
+            part[i * GA + u] = mm(lambda j: obuf[j], i * GA + u)
+        for u in range(GA):
+            start_cols(w_xout, 0, i * GA + u, i * GA + u)
+
+    rs_loop(out_tiles, HALVES, HALVES[:1], GA, 2)
     for a in HALVES[1:]:
-        @pl.loop(0, NT)
-        def _(t):
-            core_sum(a, t)
-            xsend(a, t).start()
+        @pl.loop(0, NT // GA)
+        def _(i):
+            core_sum(a, i, GA)
+            xsend(a, i, GA).start()
 
     for i in range(3, len(loads)):
         load(i).wait()
@@ -275,13 +278,14 @@
             def _():
                 gather_forward(a, kc + 1)
             gather_wait(a, kc)
+            if a == 0:
+                for b in range(5):
+                    wait_block(20 + kc * 5 + b)
             for b in range(5):
-                slot = 20 + kc * 5 + b
-                if a == 0:
-                    wait_block(slot)
-                qacc[b, rows, :] += mm(lambda j: hbuf[kc * 5 + j, rows, :], slot)
-                if last:
-                    start_cols(w_up, 0, kc * 5 + b, slot)
+                qacc[b, rows, :] += mm(lambda j: hbuf[kc * 5 + j, rows, :], 20 + kc * 5 + b)
+            if last:
+                for b in range(5):
+                    start_cols(w_up, 0, kc * 5 + b, 20 + kc * 5 + b)
 
         @pl.loop(0, HL // 2)
         def _(b):
@@ -289,14 +293,17 @@
                 qh = qacc[b, rows, 128 * hh:128 * (hh + 1)].astype(BF16)
                 obuf[b, rows, 128 * hh:128 * (hh + 1)] = attend(qh, kvx, 2 * b + hh)
 
-        def xout_tile(t):
+        def xout_tiles(i):
             if a == 0:
-                wait_block(t)
-            part[t, rows, :] = mm(lambda j: obuf[j, rows, :], t)
+                for u in range(GA):
+                    wait_block(i * GA + u)
+            for u in range(GA):
+                part[i * GA + u, rows, :] = mm(lambda j: obuf[j, rows, :], i * GA + u)
             if last:
-                start_cols(w_up, 1, t, t)
-
-        rs_loop(xout_tile, (a,), (a,), 4, 2)
+                for u in range(GA):
+                    start_cols(w_up, 1, i * GA + u, i * GA + u)
+
+        rs_loop(xout_tiles, (a,), (a,), GA, 2)
 
     for a in HALVES:
         norm_and_send(a, None, False, 3, 4)
@@ -316,8 +323,9 @@
         @pl.loop(0, NT // 4)
         def _(i):
             for u in range(4):
+                wait_block(base + i * 4 + u)
+            for u in range(4):
                 nb = i * 4 + u
-                wait_block(base + nb)
                 acc = mm(lambda j: hbuf[kc * 5 + j], base + nb)
                 if kc > 0:
                     acc = part[nb] + acc
@@ -325,27 +333,35 @@
                     part[nb] = acc
                 else:
                     ubuf[nb] = jax.nn.gelu(acc, approximate=True).astype(BF16)
+            for u in range(4):
+                nb = i * 4 + u
                 if kc < 2:
                     start_cols(w_up, kc + 2, nb, base + nb)
                 else:
                     start_down(kc - 2, nb, base + nb)
 
-    def down_tile(t):
-        g = t // 5
-        base = 20 * ((g + 1) % 2) + 4 * (t % 5)
-        acc = None
-        for kc in range(KC):
-            wait_block(base + kc)
-            new = mm(lambda j: ubuf[5 * kc + j], base + kc)
-            acc = new if acc is None else acc + new
-        part[t] = acc
-
-        @pl.when(g < 2)
-        def _():
+    def down_tiles(i):
+        def slot(t, kc):
+            return 20 * ((t // 5 + 1) % 2) + 4 * (t % 5) + kc
+
+        for u in range(GD):
             for kc in range(KC):
-                start_cols(w_down, kc, t + 10, base + kc)
-
-    rs_loop(down_tile, HALVES, HALVES, 1, 2)
+                wait_block(slot(i * GD + u, kc))
+        for u in range(GD):
+            t = i * GD + u
+            acc = mm(lambda j: ubuf[j], slot(t, 0))
+            for kc in range(1, KC):
+                acc = acc + mm(lambda j: ubuf[5 * kc + j], slot(t, kc))
+            part[t] = acc
+        for u in range(GD):
+            t = i * GD + u
+
+            @pl.when(t < 10)
+            def _():
+                for kc in range(KC):
+                    start_cols(w_down, kc, t + 10, slot(t, kc))
+
+    rs_loop(down_tiles, HALVES, HALVES, GD, 1)
 
     def out_copy(a, peer, k, core, chip):
         ref = obout.at[hrows(core, chip, a), :]
@@ -353,7 +369,7 @@
                                             device_id=peer, device_id_type=MESH)
 
     for a in HALVES:
-        mean, inv = stats(a, residual(a, 5, False))
+        mean, inv = stats(a, residual(a, 5, False, GD))
 
         def body(i, acc):
             for u in range(4):

time: 248 us -> 211 us (0.85)
  Pallas kernels: 192 us -> 156 us
    pallas_call x1, Pallas kernels: 192 us -> 156 us  [block_call(): pl.pallas_call(block_kernel, out_shape=jax.ShapeDtypeStruct((ROWS, 64), F...]
  transfers between devices with their start and end apart: 1 -> 1, of which waited for: 0 -> 0; matrix products, arithmetic and copies ran while one was open for 13% -> 15% of each run, Pallas kernels for 0% -> 0%
where the time goes in v2:
time: 211 us
  Pallas kernels  156 us (74%)
  matrix products  44.5 us (21%)
  other arithmetic  5.68 us (3%)
  starting transfers between devices  3.39 us (2%)
    pallas_call x1, Pallas kernels, block_call(): pl.pallas_call(block_kernel, out_shape=jax.ShapeDtypeStruct((ROWS, 64), F...  156 us
    dot_general x1, matrix products, device_step(): jnp.einsum('td,dchk->tchk', context, w_xkv[0], preferred_element_type=F32)  22.4 us
    dot_general x1, matrix products, device_step(): jnp.einsum('sd,dchk->schk', h_in, w_qkv[0][:, 1:3], preferred_element_typ...  12.6 us
    dot_general x1, matrix products, device_step(): jnp.einsum('sd,dhk->shk', h_in, w_qkv[0][:, 0], preferred_element_type=F32)  9.48 us
  transfers between devices with their start and end apart: 1, of which 0 were waited for; matrix products, arithmetic and copies ran while one was open for 15% of the time, Pallas kernels for 0%

profile of v2, /device:TPU:0, one launch (start us, length us, event | category | flops | bytes accessed | tf_op | source)
XLA Modules:
  0.0 211.1 jit_solution(6433954170887172631)
XLA Ops:
  0.0 0.0 copy-start
  0.0 2.3 %convert_reduce_fusion = f32[256]{0:T(256)S(1)} fusion(bf16[256,5120]{1,0:T(8,128)(2,1)} %tok_hbm.1), kind=kLoop, calls=%fused_computation.7 | loop fusion | flops 2621184 | bytes 2622464 | tf_op jit(solution)/shard_map/reduce_sum | solution.py:429
  2.3 2.6 %fusion.7 = f32[256]{0:T(256)S(1)} fusion(bf16[256,5120]{1,0:T(8,128)(2,1)} %tok_hbm.1, f32[256]{0:T(256)S(1)} %broadcast_multiply_fusion), kind=kLoop, calls=%fused_computation.10 | loop fusion | flops 5242624 | bytes 2623488 | tf_op jit(solution)/shard_map/reduce_sum | solution.py:431
  4.9 0.8 slice_add_fusion
  5.7 0.0 copy-done
  5.7 12.6 %fusion.23.kv_hbm = bf16[2,10,256,128]{3,2,1,0:T(8,128)(2,1)S(1)} fusion(bf16[5120,3,10,128]{3,0,2,1:T(8,128)(2,1)} %bitcast.60, bf16[256,5120]{1,0:T(8,128)(2,1)S(1)} %copy-done, f32[5120]{0:T(1024)S(1)} %bitcast.58, f32[5120]{0:T(1024)S(1)} %bitcast.56, f32[256]{0:T(256)S(1)} %add_rsqrt_fusion, f32[256]{0:T(256)S(1)} %broadcast_multiply_fusion), kind=kOutput, calls=%fused_computation.19 | convolution fusion | flops 6719406080 | bytes 30189568 | tf_op jit(solution)/shard_map/sd,dchk->schk/dot_general | solution.py:439
  18.3 0.0 copy-start.1
  18.3 3.4 %collective-permute-start = (bf16[2,10,256,128]{3,2,1,0:T(8,128)(2,1)S(1)}, bf16[2,10,256,128]{3,2,1,0:T(8,128)(2,1)}, u32[]{:S(2)}, u32[]{:S(2)}) collective-permute-start(bf16[2,10,256,128]{3,2,1,0:T(8,128)(2,1)S(1)} %fusion.23.kv_hbm), channel_id=1, source_target_pairs={{0,4},{4,0},{1,5},{5,1},{2,6},{6,2},{3,7},{7,3}} | collective-permute-start | bytes 3932168 | tf_op jit(solution)/shard_map/ppermute | solution.py:441
  21.7 22.4 %convert_bitcast_fusion.xkv_hbm = bf16[2,10,512,128]{3,2,1,0:T(8,128)(2,1)} fusion(bf16[5120,2,10,128]{3,1,2,0:T(2,128)(2,1)} %bitcast.62, bf16[512,5120]{1,0:T(8,128)(2,1)} %param.12), kind=kOutput, calls=%fused_computation.17 | convolution fusion | flops 13423083520 | bytes 34078720 | tf_op jit(solution)/shard_map/td,dchk->tchk/dot_general | solution.py:444
  44.1 0.0 copy-done.1
  44.1 9.5 %fusion.31.q_hbm = bf16[10,256,128]{2,1,0:T(8,128)(2,1)} fusion(bf16[5120,3,10,128]{3,0,2,1:T(8,128)(2,1)} %bitcast.61, bf16[256,5120]{1,0:T(8,128)(2,1)S(1)} %copy-done, f32[5120]{0:T(1024)S(1)} %bitcast.59, f32[5120]{0:T(1024)S(1)} %bitcast.57, f32[256]{0:T(256)S(1)} %add_rsqrt_fusion, f32[256]{0:T(256)S(1)} %broadcast_multiply_fusion), kind=kOutput, calls=%fused_computation.21 | convolution fusion | flops 3363635200 | bytes 16427008 | tf_op jit(solution)/shard_map/sd,dhk->shk/dot_general | solution.py:442
  53.6 0.0 collective-permute-done.kvo_hbm
  53.6 155.9 %dit_block.1 = f32[256,64]{1,0:T(8,128)} custom-call(bf16[10,256,128]{2,1,0:T(8,128)(2,1)} %fusion.31.q_hbm, bf16[2,10,256,128]{3,2,1,0:T(8,128)(2,1)} %copy-done.1, bf16[2,10,256,128]{3,2,1,0:T(8,128)(2,1)} %collective-permute-done.kvo_hbm, bf16[2,10,512,128]{3,2,1,0:T(8,128)(2,1)} %convert_bitcast_fusion.xkv_hbm, bf16[256,5120]{1,0:T(8,128)(2,1)} %tok_hbm.1, ...), custom_call_target="tpu_custom_call" | custom-call | flops 36864000000 | bytes 150000000 | tf_op jit(solution)/shard_map/dit_block/pallas_call | solution.py:396
  209.5 1.6 copy.13
  (2 shorter events, 0.0 us)
Async XLA Ops:
  0.0 5.7 %copy-start = (bf16[256,5120]{1,0:T(8,128)(2,1)S(1)}, bf16[256,5120]{1,0:T(8,128)(2,1)}, u32[]{:S(2)}) copy-start(bf16[256,5120]{1,0:T(8,128)(2,1)} %tok_hbm.1) | copy-start | bytes 7864324
  18.3 25.9 %copy-start.1 = (bf16[2,10,256,128]{3,2,1,0:T(8,128)(2,1)}, bf16[2,10,256,128]{3,2,1,0:T(8,128)(2,1)S(1)}, u32[]{:S(2)}) copy-start(bf16[2,10,256,128]{3,2,1,0:T(8,128)(2,1)S(1)} %fusion.23.kv_hbm) | copy-start | bytes 3932164
  18.3 35.3 %collective-permute-start = (bf16[2,10,256,128]{3,2,1,0:T(8,128)(2,1)S(1)}, bf16[2,10,256,128]{3,2,1,0:T(8,128)(2,1)}, u32[]{:S(2)}, u32[]{:S(2)}) collective-permute-start(bf16[2,10,256,128]{3,2,1,0:T(8,128)(2,1)S(1)} %fusion.23.kv_hbm), channel_id=1, source_target_pairs={{0,4},{4,0},{1,5},{5,1},{2,6},{6,2},{3,7},{7,3}} | collective-permute-start | bytes 3932168 | tf_op jit(solution)/shard_map/ppermute | solution.py:441
